TPU v7x, 64 devices: a 2x2x8 block of a 4x4x8 slice. The times are simulated.
64 devices in a mesh: rep: 8 (over x, y, core), dp: 8 (over z).
Axes of the slice: x: 2, y: 2, z: 8, core: 2. Of those that a mesh axis runs over, the one named last changes fastest.
The devices are a block of a 4x4x8 slice.
Arguments:
- x: bfloat16 [64, 4096, 640], P(('rep', 'dp')), parts along dimension 0
- dy: bfloat16 [64, 4096, 640], P(('rep', 'dp')), parts along dimension 0
- w_gate: bfloat16 [2, 640, 1536], replicated
- w_up: bfloat16 [2, 640, 1536], replicated
- w_down: bfloat16 [2, 1536, 640], replicated
- m_w_gate: float32 [2, 640, 1536], replicated
- m_w_up: float32 [2, 640, 1536], replicated
- m_w_down: float32 [2, 1536, 640], replicated
- v_w_gate: float32 [2, 640, 1536], replicated
- v_w_up: float32 [2, 640, 1536], replicated
- v_w_down: float32 [2, 1536, 640], replicated
Outputs:
- output 1: bfloat16 [16, 640, 1536], P('rep'), parts along dimension 0
- output 2: bfloat16 [16, 640, 1536], P('rep'), parts along dimension 0
- output 3: bfloat16 [16, 1536, 640], P('rep'), parts along dimension 0
- output 4: float32 [16, 640, 1536], P('rep'), parts along dimension 0
- output 5: float32 [16, 640, 1536], P('rep'), parts along dimension 0
- output 6: float32 [16, 1536, 640], P('rep'), parts along dimension 0
- output 7: float32 [16, 640, 1536], P('rep'), parts along dimension 0
- output 8: float32 [16, 640, 1536], P('rep'), parts along dimension 0
- output 9: float32 [16, 1536, 640], P('rep'), parts along dimension 0
There are 8 independent parts. A program takes and returns all parts, laid end to end along the dimension named above; an argument that names none is the same for every part.
All inputs are finite; a program needn't handle non-finite values.
Results may differ from a plain program's by a relative error of at most 0.022.
Values are sent between devices in bfloat16 or wider.
A program may use at most 768 MiB of HBM per device.

v0:
```python
import functools

import jax
import jax.numpy as jnp
from jax import lax
from jax.experimental import pallas as pl
from jax.experimental.pallas import tpu as pltpu
from jax.sharding import PartitionSpec as P


BF16, F32 = jnp.bfloat16, jnp.float32
MESH = pl.DeviceIdType.MESH
LANES = 128
BLOCK, GATHERED = 256, 4
PLAIN, BY_ROWS = ((1,), (0,)), ((1,), (1,))


def dot(a, b, contract=PLAIN):
    return lax.dot_general(a, b, (contract, ((), ())), preferred_element_type=F32)


def scale_of(wide):
    return lax.rsqrt(jnp.mean(wide * wide, -1, keepdims=True) + 1e-6)


def normed(h):
    wide = h.astype(F32)
    return (wide * scale_of(wide)).astype(BF16)


def when(condition, do):
    if isinstance(condition, bool):
        if condition:
            do()
    else:
        pl.when(condition)(do)


def at_ring(e, last):
    return 5 * e // 2 if last else 3 * e


def at_gather(e):
    return (13, 19, 25, 29, 32)[e] if e < 5 else 32 + 3 * (e - 4)


def main_kernel(
    n, x_hbm, dy_hbm, wg_hbm, wu_hbm, wd_hbm,
    g1_hbm, ga_hbm, gb_hbm, total_ref, a0t_hbm, h_hbm, dgu_hbm, gu_hbm,
    a, at, g, gt, wide, wgu, wd, acc_gu, acc_d, dgu, own, from_left, from_right, kept, squares, parts,
    x_sem, dy_sem, wide_sem, w_sem, dgu_sem, gu_sem, in_sem, send_sem, recv_sem, there_sem, here_sem, kept_sem, part_send, part_recv, credit,
):
    tokens, d = a.shape
    ff = wg_hbm.shape[2]
    block = wd.shape[1]
    blocks = ff // block
    units, half = 2 * blocks, n // 2
    tile = dgu.shape[1]
    tiles = tokens // tile
    small = tile // 2
    smalls = tokens // small
    chunk = small // 2
    chunks = tokens // chunk
    slots, shard_rows = own.shape[0], own.shape[2]
    gathered = g1_hbm.shape[1]
    me = lax.axis_index("dp")
    right, left = lax.rem(me + 1, n), lax.rem(me + n - 1, n)

    def span(i, size):
        return pl.ds(i * size, size) if isinstance(i, int) else pl.ds(pl.multiple_of(i * size, size), size)

    def dy_load(i):
        return pltpu.make_async_copy(dy_hbm.at[0, span(i, chunk)], g.at[span(i, chunk)], dy_sem.at[i])

    def wide_loads(layer):
        return [
            pltpu.make_async_copy(wg_hbm.at[layer], wide.at[:, pl.ds(0, ff)], wide_sem.at[0]),
            pltpu.make_async_copy(wu_hbm.at[layer], wide.at[:, pl.ds(ff, ff)], wide_sem.at[1]),
        ]

    def a0t_load(t):
        return pltpu.make_async_copy(a0t_hbm.at[:, span(t, tile)], at.at[:, span(t, tile)], in_sem.at[t])

    def gu_loads(b):
        slot = lax.rem(b, 2)
        return [
            pltpu.make_async_copy(ref.at[1, :, span(b, block)], wgu.at[slot, :, pl.ds(i * block, block)], w_sem.at[i, slot])
            for i, ref in enumerate((wg_hbm, wu_hbm))
        ]

    def down_load(b):
        last = jnp.int32(b < blocks) if isinstance(b, int) else (b < blocks).astype(jnp.int32)
        slot = lax.rem(b, 2)
        return pltpu.make_async_copy(wd_hbm.at[last, span(b - blocks * (1 - last), block), :], wd.at[slot], w_sem.at[2, slot])

    def ring_copy(u, k, way):
        slot = lax.rem(u, slots)
        ahead = half - k if way == 0 else n - half + k
        shard = lax.rem(me + ahead, n)
        rows = pl.ds(0, shard_rows)
        if k == 0:
            rows = pl.ds(way * (shard_rows // 2), shard_rows // 2)
        return pltpu.make_async_remote_copy(
            src_ref=own.at[slot, shard, rows],
            dst_ref=(from_left, from_right)[way].at[slot, k, rows],
            send_sem=send_sem.at[way, slot, k],
            recv_sem=recv_sem.at[way, slot, k],
            device_id={"dp": (right, left)[way]},
            device_id_type=MESH,
        )

    def ring_event(u, e, last):
        slot = lax.rem(u, slots)
        if e == 0:

            def take():
                pl.semaphore_wait(credit.at[0], 1)
                pl.semaphore_wait(credit.at[1], 1)

            when(u >= slots, take)
        else:
            for way in (0, 1):
                ring_copy(u, e - 1, way).wait()
        if 0 < e < half:
            for way in (0, 1):
                shard = lax.rem(me + (half - e if way == 0 else n - half + e), n)
                rows = pl.ds(0, shard_rows) if e > 1 else pl.ds(way * (shard_rows // 2), shard_rows // 2)
                came = (from_left, from_right)[way][slot, e - 1, rows].astype(F32)
                own[slot, shard, rows] = (own[slot, shard, rows].astype(F32) + came).astype(BF16)
        if e < half:
            for way in (0, 1):
                ring_copy(u, e, way).start()
        else:
            came = from_left[slot, e - 1].astype(F32) + from_right[slot, e - 1].astype(F32)
            done = (own[slot, me].astype(F32) + came).astype(BF16)
            kept[u] = done

            def hand_on(ref, place):
                return lambda: pltpu.make_async_copy(kept.at[u], ref.at[jnp.clip(place, 0, ref.shape[0] - 1)], kept_sem.at[u]).start()

            cut = gathered + ga_hbm.shape[0]
            when((u >= gathered) & (u < cut), hand_on(ga_hbm, u - gathered))
            if not last:
                when(u >= cut, hand_on(gb_hbm, u - cut))
            exact = done.astype(F32)
            squares[...] += jnp.sum((exact * exact).reshape(shard_rows // 8, 8, LANES), 0)

            def give():
                pl.semaphore_signal(credit.at[0], 1, device_id={"dp": left}, device_id_type=MESH)
                pl.semaphore_signal(credit.at[1], 1, device_id={"dp": right}, device_id_type=MESH)

            when(u < units - slots, give)

    def gather_copy(u, k, way):
        rows = pl.ds(0, shard_rows)
        if k == half - 1:
            rows = pl.ds(way * (shard_rows // 2), shard_rows // 2)
        place = (k, n - k)[way]
        after = (k + 1, n - k - 1)[way]
        return pltpu.make_async_remote_copy(
            src_ref=kept.at[u, rows] if k == 0 else g1_hbm.at[place, u, rows],
            dst_ref=g1_hbm.at[after, u, rows],
            send_sem=there_sem.at[way, u, k],
            recv_sem=here_sem.at[way, u, k],
            device_id={"dp": (right, left)[way]},
            device_id_type=MESH,
        )

    def kept_copy(u):
        return pltpu.make_async_copy(kept.at[u], g1_hbm.at[0, u], kept_sem.at[u])

    def gather_event(u, e):
        if e == 0:
            kept_copy(u).start()
        else:
            for way in (0, 1):
                gather_copy(u, e - 1, way).wait()
        if e < half:
            for way in (0, 1):
                gather_copy(u, e, way).start()
        else:
            kept_copy(u).wait()

    between = tiles * blocks
    second = between + smalls

    def events(now, phase, t=None):
        found = {}
        for last in (True, False):
            base, first = (0, 0) if last else (second, blocks)
            jobs = [(at_ring(e, last), blocks, functools.partial(ring_event, e=e, last=last)) for e in range(half + 1)]
            if last:
                jobs += [(at_gather(e), gathered, functools.partial(gather_event, e=e)) for e in range(half + 1)]
            for lag, count, job in jobs:
                earliest, latest = base + tiles + lag, base + tiles * count + lag
                lo, hi = ((0, between), (between, second), (second, second + between), (second + between, 1 << 30))[phase]
                if lo <= latest and earliest < hi:
                    found.setdefault(earliest % tiles, []).append((earliest, count, first, job))
        if isinstance(now, int):
            for earliest, count, first, job in found.get(now % tiles, []):
                if 0 <= now - earliest < tiles * count:
                    job(first + (now - earliest) // tiles)
            return
        for turn, some in found.items():

            @pl.when(t == turn)
            def _(some=some):
                for earliest, count, first, job in some:
                    since = now - earliest

                    @pl.when((since >= 0) & (since < tiles * count))
                    def _(job=job, since=since, first=first):
                        job(first + lax.div(since, tiles))

    def forward(x_in, a0t_out, h_out, z, gu_out, wd0):
        def x_load(i):
            slot = lax.rem(i, 4)
            return pltpu.make_async_copy(x_hbm.at[0, span(i, chunk)], x_in.at[slot], x_sem.at[slot])

        def first_stores(i):
            slot = lax.rem(i, 3)
            return [
                pltpu.make_async_copy(a0t_out.at[slot], a0t_hbm.at[:, span(i, chunk)], in_sem.at[slot]),
                pltpu.make_async_copy(gu_out.at[slot], gu_hbm.at[span(i, chunk)], gu_sem.at[slot]),
            ]

        def second_store(i):
            slot = lax.rem(i, 2)
            return pltpu.make_async_copy(h_out.at[slot], h_hbm.at[span(i, chunk)], dgu_sem.at[1, slot])

        def first(i):
            slot = lax.rem(i, 3)
            a0 = normed(x_in[lax.rem(i, 4)])
            a0t_out[slot] = a0.T
            cut = 2 * block
            for c in range(ff // cut):
                gate = dot(a0, wide[:, c * cut : (c + 1) * cut])
                up = dot(a0, wide[:, ff + c * cut : ff + (c + 1) * cut])
                gu_out[slot, :, pl.ds(c * cut, cut)] = gate
                gu_out[slot, :, pl.ds(ff + c * cut, cut)] = up
                z[lax.rem(i, 2), :, pl.ds(c * cut, cut)] = (gate * jax.nn.sigmoid(gate) * up).astype(BF16)

        def second(i):
            slot = lax.rem(i, 2)
            rows = span(i, chunk)
            h = (x_in[lax.rem(i, 4)].astype(F32) + dot(z[slot], wd0[...]).astype(BF16).astype(F32)).astype(BF16)
            h_out[slot] = h
            a1 = normed(h)
            a[rows] = a1
            at[:, rows] = a1.T
            gt[:, rows] = g[rows].T

        wd0_load = pltpu.make_async_copy(wd_hbm.at[0], wd0, wide_sem.at[2])
        x_load(0).start()
        for copy in wide_loads(0):
            copy.start()
        wd0_load.start()
        for i in (1, 2):
            x_load(i).start()
        for i in (0, 1, 2):
            dy_load(i).start()
        barrier = pltpu.get_barrier_semaphore()
        for k in range(1, n):
            pl.semaphore_signal(barrier, 1, device_id={"dp": lax.rem(me + k, n)}, device_id_type=MESH)
        squares[...] = jnp.zeros_like(squares)
        x_load(0).wait()
        for copy in wide_loads(0):
            copy.wait()
        first(0)
        for copy in first_stores(0):
            copy.start()
        wd0_load.wait()

        @pl.loop(1, chunks)
        def _(i):
            x_load(i).wait()
            dy_load(i - 1).wait()

            @pl.when(i >= 3)
            def _():
                for copy in first_stores(i - 3):
                    copy.wait()
                second_store(i - 3).wait()

            second(i - 1)
            first(i)
            for copy in first_stores(i):
                copy.start()
            second_store(i - 1).start()

            @pl.when(i + 2 < chunks)
            def _():
                dy_load(i + 2).start()
                x_load(i + 2).start()

            @pl.when(i == 1)
            def _():
                for copy in gu_loads(0):
                    copy.start()
                down_load(0).start()

        dy_load(chunks - 1).wait()
        second_store(chunks - 3).wait()
        second(chunks - 1)
        second_store(chunks - 1).start()
        for i in (chunks - 3, chunks - 2, chunks - 1):
            for copy in first_stores(i):
                copy.wait()
            if i >= chunks - 2:
                second_store(i).wait()
        pl.semaphore_wait(barrier, n - 1)

    def dgu_stores(b, t, slot):
        return [
            pltpu.make_async_copy(
                dgu.at[slot, :, pl.ds(i * block, block)],
                dgu_hbm.at[span(t, tile), pl.ds(pl.multiple_of(i * ff + b * block, block), block)],
                dgu_sem.at[i, slot],
            )
            for i in (0, 1)
        ]

    def steps(b, t, gu_in):
        rows = span(t, tile)
        slot = lax.rem(b, 2)
        gu = gu_in[lax.rem(t, 2)] if gu_in is not None else dot(a[rows], wgu[slot])
        dz = dot(g[rows], wd[slot], BY_ROWS).astype(BF16).astype(F32)
        gate, up = gu[:, :block], gu[:, block:]
        s = jax.nn.sigmoid(gate)
        silu = gate * s
        z = (silu * up).astype(BF16)
        dgate = (dz * up * (s + silu * (1 - s))).astype(BF16)
        dup = (dz * silu).astype(BF16)
        both = jnp.concatenate([dgate, dup], 1)
        if gu_in is None:
            dgu[lax.rem(t, 2)] = both
        acc_d[...] += dot(gt[:, rows], z)
        acc_gu[...] += dot(at[:, rows], both)

    def pack(b):
        slot = lax.rem(b, slots)
        of_d, of_block = d // n, block // n
        for s in range(n):
            for c in range(2 * block // LANES):
                piece = acc_gu[pl.ds(s * of_d, of_d), pl.ds(c * LANES, LANES)]
                own[slot, s, pl.ds(c * of_d, of_d)] = piece.astype(BF16)
        base = 2 * block // LANES * of_d
        for c in range(d // LANES):
            turned = acc_d[pl.ds(c * LANES, LANES)].T.astype(BF16)
            for s in range(n):
                own[slot, s, pl.ds(base + c * of_block, of_block)] = turned[s * of_block : (s + 1) * of_block]

    def clear():
        acc_gu[...] = jnp.zeros_like(acc_gu)
        acc_d[...] = jnp.zeros_like(acc_d)

    def last_block(b):
        @pl.when(b + 1 < blocks)
        def _():
            for copy in gu_loads(b + 1):
                copy.start()

        down_load(b + 1).start()
        for copy in gu_loads(b):
            copy.wait()
        down_load(b).wait()
        clear()

        @pl.loop(0, tiles)
        def _(t):
            @pl.when((b > 0) | (t > 1))
            def _():
                for copy in dgu_stores(b, t, lax.rem(t, 2)):
                    copy.wait()

            steps(b, t, None)
            for copy in dgu_stores(b, t, lax.rem(t, 2)):
                copy.start()
            events(b * tiles + t, 0, t)

        pack(b)

    def first_blocks(gu_in):
        def tile_loads(b, t):
            slot = lax.rem(t, 2)
            return [
                pltpu.make_async_copy(
                    gu_hbm.at[span(t, tile), pl.ds(pl.multiple_of(i * ff + (b - blocks) * block, block), block)],
                    gu_in.at[slot, :, pl.ds(i * block, block)],
                    dgu_sem.at[i, slot],
                )
                for i in (0, 1)
            ]

        for copy in tile_loads(blocks, 0):
            copy.start()

        @pl.loop(blocks, units)
        def _(b):
            @pl.when(b + 1 < units)
            def _():
                down_load(b + 1).start()

            down_load(b).wait()
            clear()

            @pl.loop(0, tiles)
            def _(t):
                @pl.when(b == blocks)
                def _():
                    a0t_load(t).wait()

                for copy in tile_loads(b, t):
                    copy.wait()
                ends = t == tiles - 1

                @pl.when((b + 1 < units) | jnp.logical_not(ends))
                def _():
                    for copy in tile_loads(jnp.where(ends, b + 1, b), jnp.where(ends, 0, t + 1)):
                        copy.start()

                steps(b, t, gu_in)
                events(second + (b - blocks) * tiles + t, 2, t)

            pack(b)

    def way_back(d_in, h_in):
        def in_loads(i, slot):
            return [
                pltpu.make_async_copy(dgu_hbm.at[span(i, small)], d_in.at[slot], dy_sem.at[slot]),
                pltpu.make_async_copy(h_hbm.at[span(i, small)], h_in.at[slot], dy_sem.at[2 + slot]),
            ]

        for copy in in_loads(0, 0):
            copy.start()
        for t in range(tiles):
            a0t_load(t).start()
        for copy in wide_loads(1):
            copy.wait()

        @pl.loop(0, smalls)
        def _(i):
            slot = lax.rem(i, 2)
            for copy in in_loads(i, slot):
                copy.wait()

            @pl.when(i + 1 < smalls)
            def _():
                for copy in in_loads(i + 1, 1 - slot):
                    copy.start()

            part = small // 2
            for c in range(2):
                here = pl.ds(c * part, part)
                rows = pl.ds(pl.multiple_of(i * small + c * part, part), part)
                by_a = dot(d_in[slot, here], wide[...], BY_ROWS).astype(BF16).astype(F32)
                h = h_in[slot, here].astype(F32)
                scale = scale_of(h)
                along = jnp.mean(by_a * h, -1, keepdims=True)
                by_h = (by_a * scale - h * (scale * scale * scale * along)).astype(BF16)
                out = (g[rows].astype(F32) + by_h.astype(F32)).astype(BF16)
                g[rows] = out
                gt[:, rows] = out.T
            events(between + i, 1, lax.rem(i, tiles))

    pl.run_scoped(
        forward,
        pltpu.VMEM((4, chunk, d), BF16),
        pltpu.VMEM((3, d, chunk), BF16),
        pltpu.VMEM((2, chunk, d), BF16),
        pltpu.VMEM((2, chunk, ff), BF16),
        pltpu.VMEM((3, chunk, 2 * ff), F32),
        pltpu.VMEM((ff, d), BF16),
    )
    for copy in wide_loads(1):
        copy.start()

    @pl.loop(0, blocks)
    def _(b):
        last_block(b)

    for t in (tiles - 2, tiles - 1):
        for copy in dgu_stores(blocks - 1, t, t % 2):
            copy.wait()
    pl.run_scoped(way_back, pltpu.VMEM((2, small, 2 * ff), BF16), pltpu.VMEM((2, small, d), BF16))
    pl.run_scoped(first_blocks, pltpu.VMEM((2, tile, 2 * block), F32))
    for now in range(second + between, second + between + at_ring(half, False) + 1):
        events(now, 3)

    def part_copy(k):
        return pltpu.make_async_remote_copy(
            src_ref=squares,
            dst_ref=parts.at[me],
            send_sem=part_send.at[k - 1],
            recv_sem=part_recv.at[k - 1],
            device_id={"dp": lax.rem(me + k, n)},
            device_id_type=MESH,
        )

    for k in range(1, n):
        part_copy(k).start()
    parts[me] = squares[...]
    for u in range(gathered, units):
        pltpu.make_async_copy(kept.at[u], ga_hbm.at[0], kept_sem.at[u]).wait()
    for k in range(1, n):
        part_copy(k).wait()
    total = parts[0]
    for k in range(1, n):
        total = total + parts[k]
    total_ref[...] = total


def reduced(n, x, dy, w_gate, w_up, w_down):
    tokens, d = x.shape[1:]
    ff = w_gate.shape[2]
    block, tile = BLOCK, tokens // 4
    tiles, blocks, half = tokens // tile, ff // block, n // 2
    smalls = 2 * tiles
    shard_rows = 3 * d * block // (n * LANES)
    slots = at_ring(half, False) // tiles + 1
    anywhere, vmem = pl.BlockSpec(memory_space=pl.ANY), pl.BlockSpec(memory_space=pltpu.VMEM)
    dma = pltpu.SemaphoreType.DMA
    return pl.pallas_call(
        functools.partial(main_kernel, n),
        in_specs=[anywhere] * 5,
        out_specs=[anywhere, anywhere, anywhere, vmem] + [anywhere] * 4,
        out_shape=[
            jax.ShapeDtypeStruct((n, GATHERED, shard_rows, LANES), BF16),
            jax.ShapeDtypeStruct((blocks - GATHERED // 2, shard_rows, LANES), BF16),
            jax.ShapeDtypeStruct((blocks - GATHERED // 2, shard_rows, LANES), BF16),
            jax.ShapeDtypeStruct((8, LANES), F32),
            jax.ShapeDtypeStruct((d, tokens), BF16),
            jax.ShapeDtypeStruct((tokens, d), BF16),
            jax.ShapeDtypeStruct((tokens, 2 * ff), BF16),
            jax.ShapeDtypeStruct((tokens, 2 * ff), F32),
        ],
        scratch_shapes=[
            pltpu.VMEM((tokens, d), BF16),
            pltpu.VMEM((d, tokens), BF16),
            pltpu.VMEM((tokens, d), BF16),
            pltpu.VMEM((d, tokens), BF16),
            pltpu.VMEM((d, 2 * ff), BF16),
            pltpu.VMEM((2, d, 2 * block), BF16),
            pltpu.VMEM((2, block, d), BF16),
            pltpu.VMEM((d, 2 * block), F32),
            pltpu.VMEM((d, block), F32),
            pltpu.VMEM((2, tile, 2 * block), BF16),
            pltpu.VMEM((slots, n, shard_rows, LANES), BF16),
            pltpu.VMEM((slots, half, shard_rows, LANES), BF16),
            pltpu.VMEM((slots, half, shard_rows, LANES), BF16),
            pltpu.VMEM((2 * blocks, shard_rows, LANES), BF16),
            pltpu.VMEM((8, LANES), F32),
            pltpu.VMEM((n, 8, LANES), F32),
            dma((4,)),
            dma((2 * smalls,)),
            dma((3,)),
            dma((3, 2)),
            dma((2, 2)),
            dma((3,)),
            dma((tiles,)),
            dma((2, slots, half)),
            dma((2, slots, half)),
            dma((2, GATHERED, half)),
            dma((2, GATHERED, half)),
            dma((2 * blocks,)),
            dma((n - 1,)),
            dma((n - 1,)),
            pltpu.SemaphoreType.REGULAR((2,)),
        ],
        compiler_params=pltpu.CompilerParams(collective_id=0, has_side_effects=True, vmem_limit_bytes=67_043_328),
        cost_estimate=pl.CostEstimate(flops=34 * tokens * d * ff, bytes_accessed=16 * tokens * d, transcendentals=3 * tokens * ff),
        name="reduced",
    )(x, dy, w_gate, w_up, w_down)[:4]


def update_kernel(n, pieces, count, n_terms, *refs):
    total_ref, terms, (w, m, v) = refs[0], refs[1 : 1 + n_terms], (refs[1 + n_terms + 3 * i : 4 + n_terms + 3 * i] for i in range(3))
    *refs, flat_w, tall_w, flat, tall, grads, in_sem, out_sem = refs[10 + n_terms :]
    new = [refs[len(refs) - 9 + 3 * i : len(refs) - 6 + 3 * i] for i in range(3)]
    units = grads.shape[1]
    _, _, of_d, width = flat_w.shape
    of_block, d = tall_w.shape[2:]
    block = width // units
    slabs = block // LANES
    me = lax.axis_index("dp")

    def of(k, which):
        if isinstance(k, int):
            return pieces[k][which]
        found = jnp.int32(pieces[0][which])
        for i, piece in enumerate(pieces):
            if piece[which] != pieces[i - 1][which]:
                found = jnp.where(k >= i, piece[which], found)
        return found

    def copies(k, arrays, back):
        layer, pair, shard = of(k, 0), of(k, 1), lax.rem(me + n - of(k, 2), n)
        across = pl.ds(pl.multiple_of(shard * of_d, of_d), of_d), pl.ds(pl.multiple_of(pair * width, width), width)
        pairs = []
        for kind, (first, second, third) in enumerate(arrays):
            for i, ref in enumerate((first, second)):
                pairs.append((ref.at[layer, *across], flat_w.at[k, i] if kind == 0 else flat.at[k, kind - 1, i]))
            pairs.append((third.at[layer, pl.ds(pair * units, units), shard], tall_w.at[k] if kind == 0 else tall.at[k, kind - 1]))
        sem = out_sem.at[k] if back else in_sem.at[k]
        return [pltpu.make_async_copy(*(pair[::-1] if back else pair), sem) for pair in pairs]

    def term_copy(k):
        _, _, place, term, row = pieces[k]
        ref = terms[term]
        ref = ref.at[place, pl.ds(row, units)] if len(ref.shape) == 4 else ref.at[pl.ds(row, units)]
        return pltpu.make_async_copy(ref, grads.at[k], in_sem.at[k])

    ahead = min(2, len(pieces))
    for k in range(len(pieces)):
        term_copy(k).start()
        if k < ahead:
            for copy in copies(k, (w, m, v), False):
                copy.start()
    factor = jnp.minimum(1.0, 0.5 * lax.rsqrt(jnp.sum(total_ref[...], keepdims=True) / count + 1e-30))

    @pl.loop(0, len(pieces))
    def _(k):
        @pl.when(k + ahead < len(pieces))
        def _():
            for copy in copies(k + ahead, (w, m, v), False):
                copy.start()

        pltpu.make_async_copy(grads.at[k], grads.at[k], in_sem.at[k]).wait()
        for copy in copies(k, (w, m, v), False):
            copy.wait()

        def one(w_ref, m_ref, v_ref, where, term):
            term = term.astype(F32) * factor
            m_new = 0.9 * m_ref[where] + 0.1 * term
            v_new = 0.95 * v_ref[where] + 0.05 * term * term
            wide = w_ref[where].astype(F32)
            m_ref[where] = m_new
            v_ref[where] = v_new
            w_ref[where] = (wide - 0.02 * (m_new * lax.rsqrt(v_new + 1e-8) + 0.1 * wide)).astype(BF16)

        for j in range(units):
            for i in range(2):
                for c in range(slabs):
                    where = slice(None), pl.ds(j * block + c * LANES, LANES)
                    term = grads[k, j, pl.ds((i * slabs + c) * of_d, of_d)]
                    one(flat_w.at[k, i], flat.at[k, 0, i], flat.at[k, 1, i], where, term)
            for c in range(d // LANES):
                where = j, slice(None), pl.ds(c * LANES, LANES)
                term = grads[k, j, pl.ds(2 * slabs * of_d + c * of_block, of_block)]
                one(tall_w.at[k], tall.at[k, 0], tall.at[k, 1], where, term)
        for copy in copies(k, new, True):
            copy.start()

    @pl.loop(0, len(pieces))
    def _(k):
        for copy in copies(k, new, True):
            copy.wait()


def update(pieces, terms, total, weights, m, v, so_far):
    _, d, _ = weights[0].shape
    _, _, n, of_block, _ = weights[2].shape
    of_d, units, width, n_pieces = d // n, 2, 2 * BLOCK, len(pieces)
    arrays = [*weights, *m, *v]
    aliased = list(so_far) if so_far is not None else []
    start = 1 + len(terms) + len(arrays)
    bytes_accessed = n_pieces * 22 * 3 * d * width // n
    anywhere = pl.BlockSpec(memory_space=pl.ANY)
    return pl.pallas_call(
        functools.partial(update_kernel, n, pieces, 3 * weights[0].size, len(terms)),
        in_specs=[pl.BlockSpec(memory_space=pltpu.VMEM)] + [anywhere] * (len(terms) + len(arrays) + len(aliased)),
        out_specs=[anywhere] * len(arrays),
        out_shape=[jax.ShapeDtypeStruct(one.shape, one.dtype) for one in arrays],
        scratch_shapes=[
            pltpu.VMEM((n_pieces, 2, of_d, width), BF16),
            pltpu.VMEM((n_pieces, units, of_block, d), BF16),
            pltpu.VMEM((n_pieces, 2, 2, of_d, width), F32),
            pltpu.VMEM((n_pieces, 2, units, of_block, d), F32),
            pltpu.VMEM((n_pieces, units, *terms[0].shape[-2:]), BF16),
            pltpu.SemaphoreType.DMA((n_pieces,)),
            pltpu.SemaphoreType.DMA((n_pieces,)),
        ],
        input_output_aliases={start + i: i for i in range(len(aliased))},
        compiler_params=pltpu.CompilerParams(vmem_limit_bytes=67_043_328),
        cost_estimate=pl.CostEstimate(flops=300 * bytes_accessed, bytes_accessed=bytes_accessed, transcendentals=0),
        name="update",
    )(total, *terms, *arrays, *aliased)


def solution(mesh):
    n = mesh.shape["dp"]
    half = n // 2

    def step(x, dy, *arrays):
        weights, m, v = (list(arrays[i : i + 3]) for i in (0, 3, 6))
        g1, ga, gb, total = reduced(n, x, dy, *weights)

        layers, ff, d = weights[2].shape
        split = (layers, ff // BLOCK, n, BLOCK // n, d)
        for group in (weights, m, v):
            group[2] = group[2].reshape(split)

        def sent(value, by):
            return lax.ppermute(value, "dp", [(i, (i + by) % n) for i in range(n)])

        rest = weights, m, v
        pairs = ff // (2 * BLOCK)
        here = GATHERED // 2
        each = ga.shape[0] // 2
        came = {("a", 0): [(0, ga)], ("b", 0): [(0, gb)]}
        for k in range(1, half):
            for which in "ab":
                right, left = came[which, k - 1][0][1], came[which, k - 1][-1][1]
                came[which, k] = [(k, sent(right, 1)), (n - k, sent(left, -1))]
        came["a", half] = [(half, sent(came["a", half - 1][0][1], 1))]
        came["b", half] = [(half, sent(came["b", half - 1][1][1], -1))]

        jobs = [(range(0, 2), ["a0", "b0"]), (range(2, n - 2), []), (range(n - 2, n), ["a1"])]
        jobs += [((), [f"b{k - 1}", f"a{k}"] if k < 3 else [f"b{k - 1}"]) for k in range(2, half)]
        jobs += [((), [f"a{half - 1}"]), ((), [f"b{half - 1}"]), ((), [f"a{half}", f"b{half}"])]
        out = None
        for places, names in jobs:
            terms, pieces = [g1] if places else [], [(1, pair, place, 0, 2 * pair) for place in places for pair in range(here)]
            for name in names:
                for place, array in came[name[0], int(name[1:])]:
                    for i in range(each):
                        pair = here + i + (each if name[0] == "b" else 0)
                        pieces.append((1 if pair < pairs else 0, pair % pairs, place, len(terms), 2 * i))
                    terms.append(array)
            out = update(pieces, terms, total, *rest, out)
        out = list(out)
        for i in (2, 5, 8):
            out[i] = out[i].reshape(layers, ff, d)
        return tuple(out)

    return jax.shard_map(
        step,
        mesh=mesh,
        in_specs=(P(("rep", "dp"), None, None),) * 2 + (P(None, None, None),) * 9,
        out_specs=(P("rep", None, None),) * 9,
        check_vma=False,
    )
```

profile of v0, /device:TPU:28, one launch (start us, length us, event | category | flops | bytes accessed | tf_op | source)
XLA Modules:
  0.0 324.1 jit_solution(2577644491996364738)
XLA Ops:
  0.6 232.6 %reduced.1 = (bf16[8,4,480,128]{3,2,1,0:T(8,128)(2,1)}, bf16[4,480,128]{2,1,0:T(8,128)(2,1)}, bf16[4,480,128]{2,1,0:T(8,128)(2,1)}, f32[8,128]{1,0:T(8,128)}, bf...) custom-call(bf16[1,4096,640]{2,1,0:T(8,128)(2,1)} %x_hbm.1, ...), custom_call_target="tpu_custom_call" | custom-call | flops 136902082560 | bytes 41943040 | tf_op jit(solution)/shard_map/reduced/pallas_call | solution.py:523
  233.2 1.4 collective-permute-start
  234.6 1.9 collective-permute-start.11
  236.6 0.3 collective-permute-start.4
  236.8 1.8 collective-permute-start.8
  238.6 9.5 %update.8 = (bf16[2,640,1536]{2,1,0:T(8,128)(2,1)}, bf16[2,640,1536]{2,1,0:T(8,128)(2,1)}, bf16[2,6,8,32,640]{4,3,2,1,0:T(8,128)(2,1)}, f32[2,640,1536]{2,1,0:T(...) custom-call(f32[8,128]{1,0:T(8,128)} %get-tuple-element.85.refs_0_, ...), custom_call_target="tpu_custom_call" | custom-call | flops 6488064000 | bytes 21626880 | tf_op jit(solution)/shard_map/update/pallas_call | solution.py:669
  248.1 9.5 %update.9 = (bf16[2,640,1536]{2,1,0:T(8,128)(2,1)}, bf16[2,640,1536]{2,1,0:T(8,128)(2,1)}, bf16[2,6,8,32,640]{4,3,2,1,0:T(8,128)(2,1)}, f32[2,640,1536]{2,1,0:T(...) custom-call(f32[8,128]{1,0:T(8,128)} %get-tuple-element.85.refs_0_, ...), custom_call_target="tpu_custom_call", output_to_operand_aliasing={{0}: (11, {}), {1}: (12, {}), {2}: (13, {}), {3}: (14, {}),... | custom-call | flops 6488064000 | bytes 21626880 | tf_op jit(solution)/shard_map/update/pallas_call | solution.py:669
  257.6 0.0 collective-permute-done.refs_2_
  257.6 0.2 collective-permute-start.1
  257.8 0.0 collective-permute-done.11.refs_3_
  257.8 3.1 collective-permute-start.12
  261.0 0.0 collective-permute-done.4.refs_2_
  261.0 0.3 collective-permute-start.5
  261.2 0.0 collective-permute-done.8.refs_1_
  261.2 1.8 collective-permute-start.9
  263.0 9.5 %update.10 = (bf16[2,640,1536]{2,1,0:T(8,128)(2,1)}, bf16[2,640,1536]{2,1,0:T(8,128)(2,1)}, bf16[2,6,8,32,640]{4,3,2,1,0:T(8,128)(2,1)}, f32[2,640,1536]{2,1,0:T...) custom-call(f32[8,128]{1,0:T(8,128)} %get-tuple-element.85.refs_0_, ...), custom_call_target="tpu_custom_call", output_to_operand_aliasing={{0}: (13, {}), {1}: (14, {}), {2}: (15, {}), {3}: (16, {}),... | custom-call | flops 6488064000 | bytes 21626880 | tf_op jit(solution)/shard_map/update/pallas_call | solution.py:669
  272.5 0.4 collective-permute-done.1.refs_3_
  272.9 0.0 collective-permute-start.2
  272.9 0.0 collective-permute-done.12.refs_4_
  272.9 3.2 collective-permute-start.13
  276.2 6.6 %collective-permute-done.5.refs_2_ = bf16[4,480,128]{2,1,0:T(8,128)(2,1)} collective-permute-done((bf16[4,480,128]{2,1,0:T(8,128)(2,1)}, bf16[4,480,128]{2,1,0:T(8,128)(2,1)}, u32[]{:S(2)}, u32[]{:S(2)}) %collective-permute-start.5) | collective-permute-done | bytes 491552 | tf_op jit(solution)/shard_map/ppermute | solution.py:704
  282.7 3.7 %collective-permute-start.6 = (bf16[4,480,128]{2,1,0:T(8,128)(2,1)}, bf16[4,480,128]{2,1,0:T(8,128)(2,1)}, u32[]{:S(2)}, u32[]{:S(2)}) collective-permute-start(bf16[4,480,128]{2,1,0:T(8,128)(2,1)} %collective-permute-done.5.refs_2_), channel_id=1, source_target_pairs={{0,7},{1,0},{2,1},{3,2},{4,3},{5,4},{6,5},{7,6},{8,15},{9,8},{10,9... | collective-permute-start | bytes 1474568 | tf_op jit(solution)/shard_map/ppermute | solution.py:704
  286.4 0.0 collective-permute-done.9.refs_1_
  286.4 0.0 collective-permute-start.10
  286.4 9.5 %update.11 = (bf16[2,640,1536]{2,1,0:T(8,128)(2,1)}, bf16[2,640,1536]{2,1,0:T(8,128)(2,1)}, bf16[2,6,8,32,640]{4,3,2,1,0:T(8,128)(2,1)}, f32[2,640,1536]{2,1,0:T...) custom-call(f32[8,128]{1,0:T(8,128)} %get-tuple-element.85.refs_0_, ...), custom_call_target="tpu_custom_call", output_to_operand_aliasing={{0}: (14, {}), {1}: (15, {}), {2}: (16, {}), {3}: (17, {}),... | custom-call | flops 6488064000 | bytes 21626880 | tf_op jit(solution)/shard_map/update/pallas_call | solution.py:669
  295.9 6.1 %update.12 = (bf16[2,640,1536]{2,1,0:T(8,128)(2,1)}, bf16[2,640,1536]{2,1,0:T(8,128)(2,1)}, bf16[2,6,8,32,640]{4,3,2,1,0:T(8,128)(2,1)}, f32[2,640,1536]{2,1,0:T...) custom-call(f32[8,128]{1,0:T(8,128)} %get-tuple-element.85.refs_0_, ...), custom_call_target="tpu_custom_call", output_to_operand_aliasing={{0}: (12, {}), {1}: (13, {}), {2}: (14, {}), {3}: (15, {}),... | custom-call | flops 3244032000 | bytes 10813440 | tf_op jit(solution)/shard_map/update/pallas_call | solution.py:669
  302.1 0.0 collective-permute-done.2.refs_1_
  302.1 0.3 collective-permute-start.3
  302.4 0.0 collective-permute-done.6.refs_2_
  302.4 3.2 collective-permute-start.7
  305.6 0.0 collective-permute-done.13.refs_2_
  305.6 6.1 %update.13 = (bf16[2,640,1536]{2,1,0:T(8,128)(2,1)}, bf16[2,640,1536]{2,1,0:T(8,128)(2,1)}, bf16[2,6,8,32,640]{4,3,2,1,0:T(8,128)(2,1)}, f32[2,640,1536]{2,1,0:T...) custom-call(f32[8,128]{1,0:T(8,128)} %get-tuple-element.85.refs_0_, ...), custom_call_target="tpu_custom_call", output_to_operand_aliasing={{0}: (12, {}), {1}: (13, {}), {2}: (14, {}), {3}: (15, {}),... | custom-call | flops 3244032000 | bytes 10813440 | tf_op jit(solution)/shard_map/update/pallas_call | solution.py:669
  311.6 0.0 collective-permute-done.10.refs_1_
  311.7 6.1 %update.14 = (bf16[2,640,1536]{2,1,0:T(8,128)(2,1)}, bf16[2,640,1536]{2,1,0:T(8,128)(2,1)}, bf16[2,6,8,32,640]{4,3,2,1,0:T(8,128)(2,1)}, f32[2,640,1536]{2,1,0:T...) custom-call(f32[8,128]{1,0:T(8,128)} %get-tuple-element.85.refs_0_, ...), custom_call_target="tpu_custom_call", output_to_operand_aliasing={{0}: (12, {}), {1}: (13, {}), {2}: (14, {}), {3}: (15, {}),... | custom-call | flops 3244032000 | bytes 10813440 | tf_op jit(solution)/shard_map/update/pallas_call | solution.py:669
  317.8 0.0 collective-permute-done.3.refs_1_
  317.8 0.0 collective-permute-done.7.refs_2_
  317.8 6.1 %update.15 = (bf16[2,640,1536]{2,1,0:T(8,128)(2,1)}, bf16[2,640,1536]{2,1,0:T(8,128)(2,1)}, bf16[2,6,8,32,640]{4,3,2,1,0:T(8,128)(2,1)}, f32[2,640,1536]{2,1,0:T...) custom-call(f32[8,128]{1,0:T(8,128)} %get-tuple-element.85.refs_0_, ...), custom_call_target="tpu_custom_call", output_to_operand_aliasing={{0}: (12, {}), {1}: (13, {}), {2}: (14, {}), {3}: (15, {}),... | custom-call | flops 3244032000 | bytes 10813440 | tf_op jit(solution)/shard_map/update/pallas_call | solution.py:669
Async XLA Ops:
  233.2 24.4 %collective-permute-start = (bf16[4,480,128]{2,1,0:T(8,128)(2,1)}, bf16[4,480,128]{2,1,0:T(8,128)(2,1)}, u32[]{:S(2)}, u32[]{:S(2)}) collective-permute-start(bf16[4,480,128]{2,1,0:T(8,128)(2,1)} %get-tuple-element.86.refs_2_), channel_id=1, source_target_pairs={{0,1},{1,2},{2,3},{3,4},{4,5},{5,6},{6,7},{7,0},{8,9},{9,10},{10,1... | collective-permute-start | bytes 1474568 | tf_op jit(solution)/shard_map/ppermute | solution.py:704
  234.6 23.2 %collective-permute-start.11 = (bf16[4,480,128]{2,1,0:T(8,128)(2,1)}, bf16[4,480,128]{2,1,0:T(8,128)(2,1)}, u32[]{:S(2)}, u32[]{:S(2)}) collective-permute-start(bf16[4,480,128]{2,1,0:T(8,128)(2,1)} %get-tuple-element.86.refs_2_), channel_id=1, source_target_pairs={{0,7},{1,0},{2,1},{3,2},{4,3},{5,4},{6,5},{7,6},{8,15},{9,8},{10,9... | collective-permute-start | bytes 1474568 | tf_op jit(solution)/shard_map/ppermute | solution.py:704
  236.6 24.4 %collective-permute-start.4 = (bf16[4,480,128]{2,1,0:T(8,128)(2,1)}, bf16[4,480,128]{2,1,0:T(8,128)(2,1)}, u32[]{:S(2)}, u32[]{:S(2)}) collective-permute-start(bf16[4,480,128]{2,1,0:T(8,128)(2,1)} %get-tuple-element.87.refs_3_), channel_id=1, source_target_pairs={{0,7},{1,0},{2,1},{3,2},{4,3},{5,4},{6,5},{7,6},{8,15},{9,8},{10,9... | collective-permute-start | bytes 1474568 | tf_op jit(solution)/shard_map/ppermute | solution.py:704
  236.8 24.4 %collective-permute-start.8 = (bf16[4,480,128]{2,1,0:T(8,128)(2,1)}, bf16[4,480,128]{2,1,0:T(8,128)(2,1)}, u32[]{:S(2)}, u32[]{:S(2)}) collective-permute-start(bf16[4,480,128]{2,1,0:T(8,128)(2,1)} %get-tuple-element.87.refs_3_), channel_id=1, source_target_pairs={{0,1},{1,2},{2,3},{3,4},{4,5},{5,6},{6,7},{7,0},{8,9},{9,10},{10,1... | collective-permute-start | bytes 1474568 | tf_op jit(solution)/shard_map/ppermute | solution.py:704
  257.6 15.3 %collective-permute-start.1 = (bf16[4,480,128]{2,1,0:T(8,128)(2,1)}, bf16[4,480,128]{2,1,0:T(8,128)(2,1)}, u32[]{:S(2)}, u32[]{:S(2)}) collective-permute-start(bf16[4,480,128]{2,1,0:T(8,128)(2,1)} %collective-permute-done.refs_2_), channel_id=1, source_target_pairs={{0,1},{1,2},{2,3},{3,4},{4,5},{5,6},{6,7},{7,0},{8,9},{9,10},{10,1... | collective-permute-start | bytes 1474568 | tf_op jit(solution)/shard_map/ppermute | solution.py:704
  257.8 15.1 %collective-permute-start.12 = (bf16[4,480,128]{2,1,0:T(8,128)(2,1)}, bf16[4,480,128]{2,1,0:T(8,128)(2,1)}, u32[]{:S(2)}, u32[]{:S(2)}) collective-permute-start(bf16[4,480,128]{2,1,0:T(8,128)(2,1)} %collective-permute-done.11.refs_3_), channel_id=1, source_target_pairs={{0,7},{1,0},{2,1},{3,2},{4,3},{5,4},{6,5},{7,6},{8,15},{9,8},{10,9... | collective-permute-start | bytes 1474568 | tf_op jit(solution)/shard_map/ppermute | solution.py:704
  261.0 21.8 %collective-permute-start.5 = (bf16[4,480,128]{2,1,0:T(8,128)(2,1)}, bf16[4,480,128]{2,1,0:T(8,128)(2,1)}, u32[]{:S(2)}, u32[]{:S(2)}) collective-permute-start(bf16[4,480,128]{2,1,0:T(8,128)(2,1)} %collective-permute-done.4.refs_2_), channel_id=1, source_target_pairs={{0,7},{1,0},{2,1},{3,2},{4,3},{5,4},{6,5},{7,6},{8,15},{9,8},{10,9... | collective-permute-start | bytes 1474568 | tf_op jit(solution)/shard_map/ppermute | solution.py:704
  261.2 25.2 %collective-permute-start.9 = (bf16[4,480,128]{2,1,0:T(8,128)(2,1)}, bf16[4,480,128]{2,1,0:T(8,128)(2,1)}, u32[]{:S(2)}, u32[]{:S(2)}) collective-permute-start(bf16[4,480,128]{2,1,0:T(8,128)(2,1)} %collective-permute-done.8.refs_1_), channel_id=1, source_target_pairs={{0,1},{1,2},{2,3},{3,4},{4,5},{5,6},{6,7},{7,0},{8,9},{9,10},{10,1... | collective-permute-start | bytes 1474568 | tf_op jit(solution)/shard_map/ppermute | solution.py:704
  272.9 29.2 %collective-permute-start.2 = (bf16[4,480,128]{2,1,0:T(8,128)(2,1)}, bf16[4,480,128]{2,1,0:T(8,128)(2,1)}, u32[]{:S(2)}, u32[]{:S(2)}) collective-permute-start(bf16[4,480,128]{2,1,0:T(8,128)(2,1)} %collective-permute-done.1.refs_3_), channel_id=1, source_target_pairs={{0,1},{1,2},{2,3},{3,4},{4,5},{5,6},{6,7},{7,0},{8,9},{9,10},{10,1... | collective-permute-start | bytes 1474568 | tf_op jit(solution)/shard_map/ppermute | solution.py:704
  272.9 32.6 %collective-permute-start.13 = (bf16[4,480,128]{2,1,0:T(8,128)(2,1)}, bf16[4,480,128]{2,1,0:T(8,128)(2,1)}, u32[]{:S(2)}, u32[]{:S(2)}) collective-permute-start(bf16[4,480,128]{2,1,0:T(8,128)(2,1)} %collective-permute-done.12.refs_4_), channel_id=1, source_target_pairs={{0,7},{1,0},{2,1},{3,2},{4,3},{5,4},{6,5},{7,6},{8,15},{9,8},{10,9... | collective-permute-start | bytes 1474568 | tf_op jit(solution)/shard_map/ppermute | solution.py:704
  282.7 19.7 %collective-permute-start.6 = (bf16[4,480,128]{2,1,0:T(8,128)(2,1)}, bf16[4,480,128]{2,1,0:T(8,128)(2,1)}, u32[]{:S(2)}, u32[]{:S(2)}) collective-permute-start(bf16[4,480,128]{2,1,0:T(8,128)(2,1)} %collective-permute-done.5.refs_2_), channel_id=1, source_target_pairs={{0,7},{1,0},{2,1},{3,2},{4,3},{5,4},{6,5},{7,6},{8,15},{9,8},{10,9... | collective-permute-start | bytes 1474568 | tf_op jit(solution)/shard_map/ppermute | solution.py:704
  286.4 25.2 %collective-permute-start.10 = (bf16[4,480,128]{2,1,0:T(8,128)(2,1)}, bf16[4,480,128]{2,1,0:T(8,128)(2,1)}, u32[]{:S(2)}, u32[]{:S(2)}) collective-permute-start(bf16[4,480,128]{2,1,0:T(8,128)(2,1)} %collective-permute-done.9.refs_1_), channel_id=1, source_target_pairs={{0,1},{1,2},{2,3},{3,4},{4,5},{5,6},{6,7},{7,0},{8,9},{9,10},{10,1... | collective-permute-start | bytes 1474568 | tf_op jit(solution)/shard_map/ppermute | solution.py:704
  302.1 15.7 %collective-permute-start.3 = (bf16[4,480,128]{2,1,0:T(8,128)(2,1)}, bf16[4,480,128]{2,1,0:T(8,128)(2,1)}, u32[]{:S(2)}, u32[]{:S(2)}) collective-permute-start(bf16[4,480,128]{2,1,0:T(8,128)(2,1)} %collective-permute-done.2.refs_1_), channel_id=1, source_target_pairs={{0,1},{1,2},{2,3},{3,4},{4,5},{5,6},{6,7},{7,0},{8,9},{9,10},{10,1... | collective-permute-start | bytes 1474568 | tf_op jit(solution)/shard_map/ppermute | solution.py:704
  302.4 15.4 %collective-permute-start.7 = (bf16[4,480,128]{2,1,0:T(8,128)(2,1)}, bf16[4,480,128]{2,1,0:T(8,128)(2,1)}, u32[]{:S(2)}, u32[]{:S(2)}) collective-permute-start(bf16[4,480,128]{2,1,0:T(8,128)(2,1)} %collective-permute-done.6.refs_2_), channel_id=1, source_target_pairs={{0,7},{1,0},{2,1},{3,2},{4,3},{5,4},{6,5},{7,6},{8,15},{9,8},{10,9... | collective-permute-start | bytes 1474568 | tf_op jit(solution)/shard_map/ppermute | solution.py:704
where the time goes:
time: 325 us; the launch traced here: 324 us
  Pallas kernels  295 us (91%)
  starting transfers between devices  21.1 us (6%)
  waiting for transfers between devices  7.02 us (2%)
    pallas_call x1, Pallas kernels, reduced(): pl.pallas_call(functools.partial(main_kernel, n), in_specs=[anywhere] * 5...  233 us
    pallas_call x8, Pallas kernels, update(): pl.pallas_call(functools.partial(update_kernel, n, pieces, 3 * weights[0]...  62.5 us
    ppermute x14, starting transfers between devices, sent(): return lax.ppermute(value, 'dp', [(i, (i + by) % n) for i in range(n)])  21.1 us
    ppermute x14, waiting for transfers between devices, sent(): return lax.ppermute(value, 'dp', [(i, (i + by) % n) for i in range(n)])  7.02 us
  transfers between devices with their start and end apart: 14, of which 2 were waited for; matrix products, arithmetic and copies ran while one was open for 0% of the time, Pallas kernels for 17%

commit v1 on v0

--- a/solution.py
+++ b/solution.py
@@ -46,9 +46,9 @@
 
 def main_kernel(
     n, x_hbm, dy_hbm, wg_hbm, wu_hbm, wd_hbm,
-    g1_hbm, ga_hbm, gb_hbm, total_ref, a0t_hbm, h_hbm, dgu_hbm, gu_hbm,
+    g1_hbm, ga_hbm, gb_hbm, right_hbm, left_hbm, total_ref, a0t_hbm, h_hbm, dgu_hbm, gu_hbm,
     a, at, g, gt, wide, wgu, wd, acc_gu, acc_d, dgu, own, from_left, from_right, kept, squares, parts,
-    x_sem, dy_sem, wide_sem, w_sem, dgu_sem, gu_sem, in_sem, send_sem, recv_sem, there_sem, here_sem, kept_sem, part_send, part_recv, credit,
+    x_sem, dy_sem, wide_sem, w_sem, dgu_sem, gu_sem, in_sem, send_sem, recv_sem, there_sem, here_sem, kept_sem, go_sem, come_sem, part_send, part_recv, credit,
 ):
     tokens, d = a.shape
     ff = wg_hbm.shape[2]
@@ -165,6 +165,19 @@
             device_id={"dp": (right, left)[way]},
             device_id_type=MESH,
         )
+
+    def first_step(i):
+        return [
+            pltpu.make_async_remote_copy(
+                src_ref=kept.at[gathered + i],
+                dst_ref=(right_hbm, left_hbm)[way].at[i],
+                send_sem=go_sem.at[way, i],
+                recv_sem=come_sem.at[way, i],
+                device_id={"dp": (right, left)[way]},
+                device_id_type=MESH,
+            )
+            for way in (0, 1)
+        ]
 
     def kept_copy(u):
         return pltpu.make_async_copy(kept.at[u], g1_hbm.at[0, u], kept_sem.at[u])
@@ -484,8 +497,12 @@
             copy.wait()
     pl.run_scoped(way_back, pltpu.VMEM((2, small, 2 * ff), BF16), pltpu.VMEM((2, small, d), BF16))
     pl.run_scoped(first_blocks, pltpu.VMEM((2, tile, 2 * block), F32))
-    for now in range(second + between, second + between + at_ring(half, False) + 1):
-        events(now, 3)
+    ends, early = second + between, {at_ring(half - 2, False): 0, at_ring(half - 1, False): 1}
+    for since in range(at_ring(half, False) + 1):
+        events(ends + since, 3)
+        if since in early:
+            for copy in first_step(early[since]):
+                copy.start()
 
     def part_copy(k):
         return pltpu.make_async_remote_copy(
@@ -499,6 +516,9 @@
 
     for k in range(1, n):
         part_copy(k).start()
+    for i in range(2, ga_hbm.shape[0]):
+        for copy in first_step(i):
+            copy.start()
     parts[me] = squares[...]
     for u in range(gathered, units):
         pltpu.make_async_copy(kept.at[u], ga_hbm.at[0], kept_sem.at[u]).wait()
@@ -508,6 +528,9 @@
     for k in range(1, n):
         total = total + parts[k]
     total_ref[...] = total
+    for i in range(ga_hbm.shape[0]):
+        for copy in first_step(i):
+            copy.wait()
 
 
 def reduced(n, x, dy, w_gate, w_up, w_down):
@@ -523,11 +546,10 @@
     return pl.pallas_call(
         functools.partial(main_kernel, n),
         in_specs=[anywhere] * 5,
-        out_specs=[anywhere, anywhere, anywhere, vmem] + [anywhere] * 4,
+        out_specs=[anywhere] * 5 + [vmem] + [anywhere] * 4,
         out_shape=[
             jax.ShapeDtypeStruct((n, GATHERED, shard_rows, LANES), BF16),
-            jax.ShapeDtypeStruct((blocks - GATHERED // 2, shard_rows, LANES), BF16),
-            jax.ShapeDtypeStruct((blocks - GATHERED // 2, shard_rows, LANES), BF16),
+            *[jax.ShapeDtypeStruct((blocks - GATHERED // 2, shard_rows, LANES), BF16)] * 4,
             jax.ShapeDtypeStruct((8, LANES), F32),
             jax.ShapeDtypeStruct((d, tokens), BF16),
             jax.ShapeDtypeStruct((tokens, d), BF16),
@@ -563,6 +585,7 @@
             dma((2, GATHERED, half)),
             dma((2, GATHERED, half)),
             dma((2 * blocks,)),
+            *[dma((2, blocks - GATHERED // 2))] * 2,
             dma((n - 1,)),
             dma((n - 1,)),
             pltpu.SemaphoreType.REGULAR((2,)),
@@ -570,12 +593,12 @@
         compiler_params=pltpu.CompilerParams(collective_id=0, has_side_effects=True, vmem_limit_bytes=67_043_328),
         cost_estimate=pl.CostEstimate(flops=34 * tokens * d * ff, bytes_accessed=16 * tokens * d, transcendentals=3 * tokens * ff),
         name="reduced",
-    )(x, dy, w_gate, w_up, w_down)[:4]
+    )(x, dy, w_gate, w_up, w_down)[:6]
 
 
 def update_kernel(n, pieces, count, n_terms, *refs):
     total_ref, terms, (w, m, v) = refs[0], refs[1 : 1 + n_terms], (refs[1 + n_terms + 3 * i : 4 + n_terms + 3 * i] for i in range(3))
-    *refs, flat_w, tall_w, flat, tall, grads, in_sem, out_sem = refs[10 + n_terms :]
+    *refs, flat_w, tall_w, flat, tall, grads, squares, in_sem, out_sem = refs[10 + n_terms :]
     new = [refs[len(refs) - 9 + 3 * i : len(refs) - 6 + 3 * i] for i in range(3)]
     units = grads.shape[1]
     _, _, of_d, width = flat_w.shape
@@ -611,12 +634,15 @@
         return pltpu.make_async_copy(ref, grads.at[k], in_sem.at[k])
 
     ahead = min(2, len(pieces))
+    total_copy = pltpu.make_async_copy(total_ref, squares, out_sem.at[0])
+    total_copy.start()
     for k in range(len(pieces)):
         term_copy(k).start()
         if k < ahead:
             for copy in copies(k, (w, m, v), False):
                 copy.start()
-    factor = jnp.minimum(1.0, 0.5 * lax.rsqrt(jnp.sum(total_ref[...], keepdims=True) / count + 1e-30))
+    total_copy.wait()
+    factor = jnp.minimum(1.0, 0.5 * lax.rsqrt(jnp.sum(squares[...], keepdims=True) / count + 1e-30))
 
     @pl.loop(0, len(pieces))
     def _(k):
@@ -668,7 +694,7 @@
     anywhere = pl.BlockSpec(memory_space=pl.ANY)
     return pl.pallas_call(
         functools.partial(update_kernel, n, pieces, 3 * weights[0].size, len(terms)),
-        in_specs=[pl.BlockSpec(memory_space=pltpu.VMEM)] + [anywhere] * (len(terms) + len(arrays) + len(aliased)),
+        in_specs=[anywhere] * (1 + len(terms) + len(arrays) + len(aliased)),
         out_specs=[anywhere] * len(arrays),
         out_shape=[jax.ShapeDtypeStruct(one.shape, one.dtype) for one in arrays],
         scratch_shapes=[
@@ -677,6 +703,7 @@
             pltpu.VMEM((n_pieces, 2, 2, of_d, width), F32),
             pltpu.VMEM((n_pieces, 2, units, of_block, d), F32),
             pltpu.VMEM((n_pieces, units, *terms[0].shape[-2:]), BF16),
+            pltpu.VMEM(total.shape, F32),
             pltpu.SemaphoreType.DMA((n_pieces,)),
             pltpu.SemaphoreType.DMA((n_pieces,)),
         ],
@@ -690,10 +717,14 @@
 def solution(mesh):
     n = mesh.shape["dp"]
     half = n // 2
+    sends = [one for k in range(1, half) for one in (("a", k + 1), ("b", k))] + [("b", half)]
+
+    def ways(which, k):
+        return ("right", "left") if k < half else ("right",) if which == "a" else ("left",)
 
     def step(x, dy, *arrays):
         weights, m, v = (list(arrays[i : i + 3]) for i in (0, 3, 6))
-        g1, ga, gb, total = reduced(n, x, dy, *weights)
+        g1, ga, gb, ga_right, ga_left, total = reduced(n, x, dy, *weights)
 
         layers, ff, d = weights[2].shape
         split = (layers, ff // BLOCK, n, BLOCK // n, d)
@@ -707,17 +738,18 @@
         pairs = ff // (2 * BLOCK)
         here = GATHERED // 2
         each = ga.shape[0] // 2
-        came = {("a", 0): [(0, ga)], ("b", 0): [(0, gb)]}
-        for k in range(1, half):
-            for which in "ab":
-                right, left = came[which, k - 1][0][1], came[which, k - 1][-1][1]
-                came[which, k] = [(k, sent(right, 1)), (n - k, sent(left, -1))]
-        came["a", half] = [(half, sent(came["a", half - 1][0][1], 1))]
-        came["b", half] = [(half, sent(came["b", half - 1][1][1], -1))]
-
-        jobs = [(range(0, 2), ["a0", "b0"]), (range(2, n - 2), []), (range(n - 2, n), ["a1"])]
-        jobs += [((), [f"b{k - 1}", f"a{k}"] if k < 3 else [f"b{k - 1}"]) for k in range(2, half)]
-        jobs += [((), [f"a{half - 1}"]), ((), [f"b{half - 1}"]), ((), [f"a{half}", f"b{half}"])]
+        came = {("a", 0): [(0, ga)], ("b", 0): [(0, gb)], ("a", 1): [(1, ga_right), (n - 1, ga_left)]}
+        for which, k in sends:
+            right, left = came[which, k - 1][0][1], came[which, k - 1][-1][1]
+            came[which, k] = [
+                (k if by > 0 else n - k, sent(one, by))
+                for one, by, way in ((right, 1, "right"), (left, -1, "left"))
+                if way in ways(which, k)
+            ]
+
+        jobs = [(range(0, 1), ["a0", "b0", "a1"]), (range(1, half + 1), []), (range(half + 1, n), [])]
+        jobs += [((), [f"{which}{k}" for which, k in sends[2 * i : 2 * i + 2]]) for i in range(half - 2)]
+        jobs += [((), [f"b{half - 1}", f"a{half}"]), ((), [f"b{half}"])]
         out = None
         for places, names in jobs:
             terms, pieces = [g1] if places else [], [(1, pair, place, 0, 2 * pair) for place in places for pair in range(here)]

time: 325 us -> 327 us (level)
  waiting for transfers between devices: 7.02 us -> 13.8 us
  starting transfers between devices: 21.1 us -> 16.9 us
    ppermute x14 -> x12, waiting for transfers between devices: 7.02 us -> 13.8 us  [sent(): return lax.ppermute(value, 'dp', [(i, (i + by) % n) for i in range(n)])]
    pallas_call x8 -> x7, Pallas kernels: 62.5 us -> 58.2 us  [update(): pl.pallas_call(functools.partial(update_kernel, n, pieces, 3 * weights[0]...]
    ppermute x14 -> x12, starting transfers between devices: 21.1 us -> 16.9 us  [sent(): return lax.ppermute(value, 'dp', [(i, (i + by) % n) for i in range(n)])]
    pallas_call x1, Pallas kernels: 233 us -> 237 us  [reduced(): pl.pallas_call(functools.partial(main_kernel, n), in_specs=[anywhere] * 5...]
  transfers between devices with their start and end apart: 14 -> 12, of which waited for: 2 -> 3; matrix products, arithmetic and copies ran while one was open for 0% -> 0% of each run, Pallas kernels for 17% -> 17%
where the time goes in v1:
time: 327 us; the launch traced here: 326 us
  Pallas kernels  295 us (90%)
  starting transfers between devices  16.9 us (5%)
  waiting for transfers between devices  13.8 us (4%)
    pallas_call x1, Pallas kernels, reduced(): pl.pallas_call(functools.partial(main_kernel, n), in_specs=[anywhere] * 5...  237 us
    pallas_call x7, Pallas kernels, update(): pl.pallas_call(functools.partial(update_kernel, n, pieces, 3 * weights[0]...  58.2 us
    ppermute x12, starting transfers between devices, sent(): return lax.ppermute(value, 'dp', [(i, (i + by) % n) for i in range(n)])  16.9 us
    ppermute x12, waiting for transfers between devices, sent(): return lax.ppermute(value, 'dp', [(i, (i + by) % n) for i in range(n)])  13.8 us
  transfers between devices with their start and end apart: 12, of which 3 were waited for; matrix products, arithmetic and copies ran while one was open for 0% of the time, Pallas kernels for 17%

profile of v1, /device:TPU:28, one launch (start us, length us, event | category | flops | bytes accessed | tf_op | source)
XLA Modules:
  0.0 326.5 jit_solution(4572827216648625979)
XLA Ops:
  0.6 236.7 %reduced.1 = (bf16[8,4,480,128]{3,2,1,0:T(8,128)(2,1)}, bf16[4,480,128]{2,1,0:T(8,128)(2,1)}, bf16[4,480,128]{2,1,0:T(8,128)(2,1)}, bf16[4,480,128]{2,1,0:T(8,12...) custom-call(bf16[1,4096,640]{2,1,0:T(8,128)(2,1)} %x_hbm.1, ...), custom_call_target="tpu_custom_call" | custom-call | flops 136902082560 | bytes 41943040 | tf_op jit(solution)/shard_map/reduced/pallas_call | solution.py:546
  237.4 1.7 collective-permute-start
  239.1 0.4 collective-permute-start.4
  239.5 2.8 collective-permute-start.10
  242.3 0.0 collective-permute-start.7
  242.4 11.2 %update.7 = (bf16[2,640,1536]{2,1,0:T(8,128)(2,1)}, bf16[2,640,1536]{2,1,0:T(8,128)(2,1)}, bf16[2,6,8,32,640]{4,3,2,1,0:T(8,128)(2,1)}, f32[2,640,1536]{2,1,0:T(...) custom-call(f32[8,128]{1,0:T(8,128)} %get-tuple-element.78.refs_0_, ...), custom_call_target="tpu_custom_call" | custom-call | flops 8110080000 | bytes 27033600 | tf_op jit(solution)/shard_map/update/pallas_call | solution.py:695
  253.5 0.0 collective-permute-done.refs_4_
  253.5 3.3 %collective-permute-start.1 = (bf16[4,480,128]{2,1,0:T(8,128)(2,1)}, bf16[4,480,128]{2,1,0:T(8,128)(2,1)}, u32[]{:S(2)}, u32[]{:S(2)}) collective-permute-start(bf16[4,480,128]{2,1,0:T(8,128)(2,1)} %collective-permute-done.refs_4_), channel_id=1, source_target_pairs={{0,7},{1,0},{2,1},{3,2},{4,3},{5,4},{6,5},{7,6},{8,15},{9,8},{10,9... | collective-permute-start | bytes 1474568 | tf_op jit(solution)/shard_map/ppermute | solution.py:735
  256.9 9.6 %update.8 = (bf16[2,640,1536]{2,1,0:T(8,128)(2,1)}, bf16[2,640,1536]{2,1,0:T(8,128)(2,1)}, bf16[2,6,8,32,640]{4,3,2,1,0:T(8,128)(2,1)}, f32[2,640,1536]{2,1,0:T(...) custom-call(f32[8,128]{1,0:T(8,128)} %get-tuple-element.78.refs_0_, ...), custom_call_target="tpu_custom_call", output_to_operand_aliasing={{0}: (11, {}), {1}: (12, {}), {2}: (13, {}), {3}: (14, {}),... | custom-call | flops 6488064000 | bytes 21626880 | tf_op jit(solution)/shard_map/update/pallas_call | solution.py:695
  266.4 7.4 %update.9 = (bf16[2,640,1536]{2,1,0:T(8,128)(2,1)}, bf16[2,640,1536]{2,1,0:T(8,128)(2,1)}, bf16[2,6,8,32,640]{4,3,2,1,0:T(8,128)(2,1)}, f32[2,640,1536]{2,1,0:T(...) custom-call(f32[8,128]{1,0:T(8,128)} %get-tuple-element.78.refs_0_, ...), custom_call_target="tpu_custom_call", output_to_operand_aliasing={{0}: (11, {}), {1}: (12, {}), {2}: (13, {}), {3}: (14, {}),... | custom-call | flops 4866048000 | bytes 16220160 | tf_op jit(solution)/shard_map/update/pallas_call | solution.py:695
  273.9 0.0 collective-permute-done.4.refs_3_
  273.9 0.1 collective-permute-start.5
  274.0 0.0 collective-permute-done.7.refs_1_
  274.0 0.1 collective-permute-start.8
  274.1 0.0 collective-permute-done.10.refs_2_
  274.2 3.2 collective-permute-start.11
  277.4 0.0 collective-permute-done.1.refs_4_
  277.4 1.9 collective-permute-start.2
  279.3 9.6 %update.10 = (bf16[2,640,1536]{2,1,0:T(8,128)(2,1)}, bf16[2,640,1536]{2,1,0:T(8,128)(2,1)}, bf16[2,6,8,32,640]{4,3,2,1,0:T(8,128)(2,1)}, f32[2,640,1536]{2,1,0:T...) custom-call(f32[8,128]{1,0:T(8,128)} %get-tuple-element.78.refs_0_, ...), custom_call_target="tpu_custom_call", output_to_operand_aliasing={{0}: (14, {}), {1}: (15, {}), {2}: (16, {}), {3}: (17, {}),... | custom-call | flops 6488064000 | bytes 21626880 | tf_op jit(solution)/shard_map/update/pallas_call | solution.py:695
  288.8 0.8 collective-permute-done.5.refs_3_
  289.6 0.0 collective-permute-start.6
  289.6 10.5 %collective-permute-done.8.refs_1_ = bf16[4,480,128]{2,1,0:T(8,128)(2,1)} collective-permute-done((bf16[4,480,128]{2,1,0:T(8,128)(2,1)}, bf16[4,480,128]{2,1,0:T(8,128)(2,1)}, u32[]{:S(2)}, u32[]{:S(2)}) %collective-permute-start.8) | collective-permute-done | bytes 491552 | tf_op jit(solution)/shard_map/ppermute | solution.py:735
  300.1 0.0 collective-permute-start.9
  300.1 0.0 collective-permute-done.2.refs_2_
  300.1 3.2 collective-permute-start.3
  303.4 0.0 collective-permute-done.11.refs_2_
  303.4 9.6 %update.11 = (bf16[2,640,1536]{2,1,0:T(8,128)(2,1)}, bf16[2,640,1536]{2,1,0:T(8,128)(2,1)}, bf16[2,6,8,32,640]{4,3,2,1,0:T(8,128)(2,1)}, f32[2,640,1536]{2,1,0:T...) custom-call(f32[8,128]{1,0:T(8,128)} %get-tuple-element.78.refs_0_, ...), custom_call_target="tpu_custom_call", output_to_operand_aliasing={{0}: (14, {}), {1}: (15, {}), {2}: (16, {}), {3}: (17, {}),... | custom-call | flops 6488064000 | bytes 21626880 | tf_op jit(solution)/shard_map/update/pallas_call | solution.py:695
  313.0 0.0 collective-permute-done.6.refs_1_
  313.0 2.5 collective-permute-done.9.refs_3_
  315.4 7.3 %update.12 = (bf16[2,640,1536]{2,1,0:T(8,128)(2,1)}, bf16[2,640,1536]{2,1,0:T(8,128)(2,1)}, bf16[2,6,8,32,640]{4,3,2,1,0:T(8,128)(2,1)}, f32[2,640,1536]{2,1,0:T...) custom-call(f32[8,128]{1,0:T(8,128)} %get-tuple-element.78.refs_0_, ...), custom_call_target="tpu_custom_call", output_to_operand_aliasing={{0}: (13, {}), {1}: (14, {}), {2}: (15, {}), {3}: (16, {}),... | custom-call | flops 4866048000 | bytes 16220160 | tf_op jit(solution)/shard_map/update/pallas_call | solution.py:695
  322.8 0.0 collective-permute-done.3.refs_1_
  322.8 3.6 %update.13 = (bf16[2,640,1536]{2,1,0:T(8,128)(2,1)}, bf16[2,640,1536]{2,1,0:T(8,128)(2,1)}, bf16[2,6,8,32,640]{4,3,2,1,0:T(8,128)(2,1)}, f32[2,640,1536]{2,1,0:T...) custom-call(f32[8,128]{1,0:T(8,128)} %get-tuple-element.78.refs_0_, ...), custom_call_target="tpu_custom_call", output_to_operand_aliasing={{0}: (11, {}), {1}: (12, {}), {2}: (13, {}), {3}: (14, {}),... | custom-call | flops 1622016000 | bytes 5406720 | tf_op jit(solution)/shard_map/update/pallas_call | solution.py:695
Async XLA Ops:
  237.4 16.1 %collective-permute-start = (bf16[4,480,128]{2,1,0:T(8,128)(2,1)}, bf16[4,480,128]{2,1,0:T(8,128)(2,1)}, u32[]{:S(2)}, u32[]{:S(2)}) collective-permute-start(bf16[4,480,128]{2,1,0:T(8,128)(2,1)} %get-tuple-element.79.refs_3_), channel_id=1, source_target_pairs={{0,7},{1,0},{2,1},{3,2},{4,3},{5,4},{6,5},{7,6},{8,15},{9,8},{10,9... | collective-permute-start | bytes 1474568 | tf_op jit(solution)/shard_map/ppermute | solution.py:735
  239.1 34.8 %collective-permute-start.4 = (bf16[4,480,128]{2,1,0:T(8,128)(2,1)}, bf16[4,480,128]{2,1,0:T(8,128)(2,1)}, u32[]{:S(2)}, u32[]{:S(2)}) collective-permute-start(bf16[4,480,128]{2,1,0:T(8,128)(2,1)} %get-tuple-element.79.refs_3_), channel_id=1, source_target_pairs={{0,1},{1,2},{2,3},{3,4},{4,5},{5,6},{6,7},{7,0},{8,9},{9,10},{10,1... | collective-permute-start | bytes 1474568 | tf_op jit(solution)/shard_map/ppermute | solution.py:735
  239.5 34.6 %collective-permute-start.10 = (bf16[4,480,128]{2,1,0:T(8,128)(2,1)}, bf16[4,480,128]{2,1,0:T(8,128)(2,1)}, u32[]{:S(2)}, u32[]{:S(2)}) collective-permute-start(bf16[4,480,128]{2,1,0:T(8,128)(2,1)} %get-tuple-element.81.refs_5_), channel_id=1, source_target_pairs={{0,7},{1,0},{2,1},{3,2},{4,3},{5,4},{6,5},{7,6},{8,15},{9,8},{10,9... | collective-permute-start | bytes 1474568 | tf_op jit(solution)/shard_map/ppermute | solution.py:735
  242.3 31.7 %collective-permute-start.7 = (bf16[4,480,128]{2,1,0:T(8,128)(2,1)}, bf16[4,480,128]{2,1,0:T(8,128)(2,1)}, u32[]{:S(2)}, u32[]{:S(2)}) collective-permute-start(bf16[4,480,128]{2,1,0:T(8,128)(2,1)} %get-tuple-element.80.refs_4_), channel_id=1, source_target_pairs={{0,1},{1,2},{2,3},{3,4},{4,5},{5,6},{6,7},{7,0},{8,9},{9,10},{10,1... | collective-permute-start | bytes 1474568 | tf_op jit(solution)/shard_map/ppermute | solution.py:735
  253.5 23.8 %collective-permute-start.1 = (bf16[4,480,128]{2,1,0:T(8,128)(2,1)}, bf16[4,480,128]{2,1,0:T(8,128)(2,1)}, u32[]{:S(2)}, u32[]{:S(2)}) collective-permute-start(bf16[4,480,128]{2,1,0:T(8,128)(2,1)} %collective-permute-done.refs_4_), channel_id=1, source_target_pairs={{0,7},{1,0},{2,1},{3,2},{4,3},{5,4},{6,5},{7,6},{8,15},{9,8},{10,9... | collective-permute-start | bytes 1474568 | tf_op jit(solution)/shard_map/ppermute | solution.py:735
  273.9 15.7 %collective-permute-start.5 = (bf16[4,480,128]{2,1,0:T(8,128)(2,1)}, bf16[4,480,128]{2,1,0:T(8,128)(2,1)}, u32[]{:S(2)}, u32[]{:S(2)}) collective-permute-start(bf16[4,480,128]{2,1,0:T(8,128)(2,1)} %collective-permute-done.4.refs_3_), channel_id=1, source_target_pairs={{0,1},{1,2},{2,3},{3,4},{4,5},{5,6},{6,7},{7,0},{8,9},{9,10},{10,1... | collective-permute-start | bytes 1474568 | tf_op jit(solution)/shard_map/ppermute | solution.py:735
  274.0 26.1 %collective-permute-start.8 = (bf16[4,480,128]{2,1,0:T(8,128)(2,1)}, bf16[4,480,128]{2,1,0:T(8,128)(2,1)}, u32[]{:S(2)}, u32[]{:S(2)}) collective-permute-start(bf16[4,480,128]{2,1,0:T(8,128)(2,1)} %collective-permute-done.7.refs_1_), channel_id=1, source_target_pairs={{0,1},{1,2},{2,3},{3,4},{4,5},{5,6},{6,7},{7,0},{8,9},{9,10},{10,1... | collective-permute-start | bytes 1474568 | tf_op jit(solution)/shard_map/ppermute | solution.py:735
  274.2 29.2 %collective-permute-start.11 = (bf16[4,480,128]{2,1,0:T(8,128)(2,1)}, bf16[4,480,128]{2,1,0:T(8,128)(2,1)}, u32[]{:S(2)}, u32[]{:S(2)}) collective-permute-start(bf16[4,480,128]{2,1,0:T(8,128)(2,1)} %collective-permute-done.10.refs_2_), channel_id=1, source_target_pairs={{0,7},{1,0},{2,1},{3,2},{4,3},{5,4},{6,5},{7,6},{8,15},{9,8},{10,9... | collective-permute-start | bytes 1474568 | tf_op jit(solution)/shard_map/ppermute | solution.py:735
  277.4 22.8 %collective-permute-start.2 = (bf16[4,480,128]{2,1,0:T(8,128)(2,1)}, bf16[4,480,128]{2,1,0:T(8,128)(2,1)}, u32[]{:S(2)}, u32[]{:S(2)}) collective-permute-start(bf16[4,480,128]{2,1,0:T(8,128)(2,1)} %collective-permute-done.1.refs_4_), channel_id=1, source_target_pairs={{0,7},{1,0},{2,1},{3,2},{4,3},{5,4},{6,5},{7,6},{8,15},{9,8},{10,9... | collective-permute-start | bytes 1474568 | tf_op jit(solution)/shard_map/ppermute | solution.py:735
  289.6 23.4 %collective-permute-start.6 = (bf16[4,480,128]{2,1,0:T(8,128)(2,1)}, bf16[4,480,128]{2,1,0:T(8,128)(2,1)}, u32[]{:S(2)}, u32[]{:S(2)}) collective-permute-start(bf16[4,480,128]{2,1,0:T(8,128)(2,1)} %collective-permute-done.5.refs_3_), channel_id=1, source_target_pairs={{0,1},{1,2},{2,3},{3,4},{4,5},{5,6},{6,7},{7,0},{8,9},{9,10},{10,1... | collective-permute-start | bytes 1474568 | tf_op jit(solution)/shard_map/ppermute | solution.py:735
  300.1 15.3 %collective-permute-start.9 = (bf16[4,480,128]{2,1,0:T(8,128)(2,1)}, bf16[4,480,128]{2,1,0:T(8,128)(2,1)}, u32[]{:S(2)}, u32[]{:S(2)}) collective-permute-start(bf16[4,480,128]{2,1,0:T(8,128)(2,1)} %collective-permute-done.8.refs_1_), channel_id=1, source_target_pairs={{0,1},{1,2},{2,3},{3,4},{4,5},{5,6},{6,7},{7,0},{8,9},{9,10},{10,1... | collective-permute-start | bytes 1474568 | tf_op jit(solution)/shard_map/ppermute | solution.py:735
  300.1 22.6 %collective-permute-start.3 = (bf16[4,480,128]{2,1,0:T(8,128)(2,1)}, bf16[4,480,128]{2,1,0:T(8,128)(2,1)}, u32[]{:S(2)}, u32[]{:S(2)}) collective-permute-start(bf16[4,480,128]{2,1,0:T(8,128)(2,1)} %collective-permute-done.2.refs_2_), channel_id=1, source_target_pairs={{0,7},{1,0},{2,1},{3,2},{4,3},{5,4},{6,5},{7,6},{8,15},{9,8},{10,9... | collective-permute-start | bytes 1474568 | tf_op jit(solution)/shard_map/ppermute | solution.py:735
